TPU v7x, 32 devices: a whole 2x2x4 slice. The times are simulated.
32 devices in a mesh: row: 8 (over z, x), col: 4 (over y, core).
Axes of the slice: x: 2, y: 2, z: 4, core: 2. Of those that a mesh axis runs over, the one named last changes fastest.
Arguments:
- prior_scores: float32 [12288, 12288], P('row', 'col'), may hold values from 0.001 to 10
- tiles_first: bfloat16 [96, 5, 128, 128], P('row'), may hold values from 0 to 1, as said below
- columns_first: int32 [96, 5], P('row'), may hold values from 0 to 95, as said below
- tiles_second: bfloat16 [96, 5, 128, 128], P('col'), may hold values from 0 to 1, as said below
- columns_second: int32 [96, 5], P('col'), may hold values from 0 to 95, as said below
Outputs:
- alignment: float32 [12288, 12288], P('row', 'col')
Inputs may be any that keep to these rules, and one draw needn't show every extreme that they name: `tiles_first`: in every block row, the block in the first slot has entries of 0.5 or more on its diagonal. `tiles_second`: in every block row, the block in the first slot has entries of 0.5 or more on its diagonal. `columns_first`: each block row lists 5 different block columns. `columns_second`: each block row lists 5 different block columns.
All inputs are finite; a program needn't handle non-finite values.
Results may differ from a plain program's by a relative error of at most 0.0004.
The roundings to bfloat16 on the way count: a program that leaves them out, or rounds other values in their place, can miss the bound.
Values may be sent and summed in bfloat16 or wider, within the bound.
A program may use at most 192 MiB of HBM per device.

v0:
```python
import jax
import jax.numpy as jnp
from jax import lax
from jax.sharding import PartitionSpec as P

ITERS = 2
mixing = 0.8


def second_product(features, tile_set, columns, inverse):
    tile_size = tile_set.shape[2]
    blocks = features.reshape(-1, tile_size, features.shape[1])
    picked = jnp.take(blocks, columns, axis=0)
    result = jnp.einsum("jsoi,jsin->jon", tile_set, picked, preferred_element_type=jnp.float32)
    result = result.reshape(-1, features.shape[1]) * inverse[:, None]
    return result.astype(jnp.bfloat16)


def first_product(slab_data, tile_set, columns, inverse):
    tile_size = tile_set.shape[2]
    blocks = slab_data.reshape(slab_data.shape[0], -1, tile_size)
    picked = jnp.take(blocks, columns, axis=1)
    result = jnp.einsum("cisk,isok->cio", picked, tile_set, preferred_element_type=jnp.float32)
    result = result.reshape(slab_data.shape[0], -1) * inverse[None, :]
    return result.astype(jnp.bfloat16)


def local(prior_scores, tiles_first, columns_first, tiles_second, columns_second):
    prior_cols = prior_scores.T
    row_count = lax.axis_size("row")
    cell_count = float(
        prior_scores.shape[0] * row_count * prior_scores.shape[1] * lax.axis_size("col")
    )
    all_first, all_columns = (
        lax.all_gather(tiles_first, "row", axis=0, tiled=True),
        lax.all_gather(columns_first, "row", axis=0, tiled=True),
    )
    inverse_first = 1.0 / jnp.sum(all_first, axis=(1, 3), dtype=jnp.float32).reshape(-1)
    inverse_second = 1.0 / jnp.sum(tiles_second, axis=(1, 3), dtype=jnp.float32).reshape(-1)
    prior_sum = lax.psum(jnp.sum(prior_cols), ("row", "col"))
    current_state = prior_cols
    for iteration in range(ITERS):
        current = current_state.astype(jnp.bfloat16)
        gathered = lax.all_gather(current, "col", axis=0, tiled=True)
        mixed_cols = second_product(gathered, tiles_second, columns_second, inverse_second)
        slab_data = lax.all_to_all(mixed_cols, "row", split_axis=0, concat_axis=1, tiled=True)
        propagated = first_product(slab_data, all_first, all_columns, inverse_first)
        partial_value = jnp.sum(propagated.astype(jnp.float32))
        returned = lax.all_to_all(propagated, "row", split_axis=1, concat_axis=0, tiled=True)
        slab_sum = lax.psum(partial_value, ("row", "col"))
        grand_total = mixing * slab_sum + (1.0 - mixing) * prior_sum
        updated = mixing * returned.astype(jnp.float32) + (1.0 - mixing) * prior_cols
        current_state = updated / (grand_total / cell_count)
    return current_state.T


def solution(mesh):
    return jax.shard_map(
        local,
        mesh=mesh,
        in_specs=(
            P("row", "col"),
            P("row", None, None, None),
            P("row", None),
            P("col", None, None, None),
            P("col", None),
        ),
        out_specs=P("row", "col"),
        check_vma=False,
    )
```

profile of v0, /device:TPU:0, one launch (start us, length us, event | category | flops | bytes accessed | tf_op | source)
XLA Modules:
  0.0 1965.2 jit_solution(3482156097374935337)
XLA Ops:
  6.5 0.0 all-gather.5.cloned.1.call-start
  6.5 20.0 %fusion.28 = (f32[]{:T(128)}, bf16[3072,1536]{0,1:T(8,128)(2,1)}) fusion(f32[1536,3072]{1,0:T(8,128)} %param.9), kind=kLoop, calls=%fused_computation.55 | loop fusion | flops 9437183 | bytes 28311556 | tf_op jit(solution)/shard_map/reduce_sum | solution.py:40
  26.5 0.0 all-gather.5.cloned.1.call-update
  26.6 0.0 all-gather.7.cloned.1.call-start
  26.6 0.7 all-gather.7.cloned.1.call-update
  27.3 0.0 copy-done.10
  27.3 0.1 copy.33
  27.5 0.1 copy.37
  27.5 0.1 reshape.154
  27.6 2.7 convert_reduce_fusion.3
  30.4 0.0 copy-start.8
  30.4 0.0 copy-start.4
  30.4 226.2 %all-gather.5.cloned.1.call-done = bf16[12288,1536]{0,1:T(8,128)(2,1)} async-done(((bf16[3072,1536]{0,1:T(8,128)(2,1)}), bf16[12288,1536]{0,1:T(8,128)(2,1)}) %all-gather.5.cloned.1.call-update) | async-done | bytes 37748752 | tf_op jit(solution)/shard_map/all_gather | solution.py:44
  256.6 48.9 %copy.36 = bf16[12288,1536]{1,0:T(8,128)(2,1)} copy(bf16[12288,1536]{0,1:T(8,128)(2,1)} %all-gather.5.cloned.1.call-done) | data formatting | bytes 75497472 | tf_op jit(solution)/shard_map/all_gather | solution.py:44
  305.6 0.0 copy-done.4
  305.6 33.3 %gather_fusion = bf16[120,128,1536]{2,1,0:T(8,128)(2,1)} fusion(bf16[96,128,1536]{2,1,0:T(8,128)(2,1)} %bitcast.87, s32[1024]{0:T(1024)S(1)} %pad_clamp_fusion.1), kind=kCustom, calls=%fused_computation.clone | custom fusion | bytes 94372320 | tf_op jit(solution)/shard_map/jit(_take)/gather | solution.py:13
  338.8 0.0 copy-done.14
  338.8 26.4 %fusion.8 = f32[24,1536,128,1]{1,2,3,0:T(8,128)} fusion(bf16[24,5,128,128]{3,2,1,0:T(8,128)(2,1)} %param.12, bf16[24,5,128,1536]{3,2,1,0:T(8,128)(2,1)} %bitcast.93, pred[24,5]{1,0:T(8,128)(4,1)S(1)} %copy.33), kind=kOutput, calls=%fused_computation.12 | convolution fusion | flops 6063390720 | bytes 69992568 | tf_op jit(solution)/shard_map/jsoi,jsin->jon/dot_general | solution.py:14
  365.2 18.7 copy.38
  383.9 0.0 copy-done.8
  383.9 11.5 multiply_convert_fusion.3
  395.4 5.4 all-to-all-start
  400.8 0.0 copy-done.13
  400.8 292.1 %all-gather = s32[8,12,5]{1,2,0:T(8,128)S(1)} all-gather(s32[1,12,5]{1,2,0:T(8,128)S(1)} %bitcast.99), channel_id=1, replica_groups=mesh['row'=8,'col'=4] {'row'}, dimensions={0}, use_global_device_ids=true | all-gather | bytes 2160 | tf_op jit(solution)/shard_map/all_gather | solution.py:36
  692.9 0.1 reshape.153
  693.0 0.1 copy.32
  693.2 0.1 copy.39
  693.3 0.2 reshape.158
  693.4 0.0 copy-start
  693.5 0.0 all-gather.7.cloned.1.call-done
  693.5 6.6 convert_reduce_fusion
  700.1 0.0 copy-start.2
  700.2 0.0 all-to-all-done
  700.2 12.6 copy.40
  712.8 23.6 %gather_fusion.1 = bf16[480,384,128]{2,1,0:T(8,128)(2,1)} fusion(bf16[384,96,128]{2,0,1:T(8,128)(2,1)} %copy.40, s32[1024]{0:T(1024)S(1)} %pad_clamp_fusion), kind=kCustom, calls=%fused_computation.1.clone | custom fusion | bytes 94373760 | tf_op jit(solution)/shard_map/jit(_take)/gather | solution.py:22
  736.4 0.0 copy-done.11
  736.4 31.3 %convert_reduce_fusion.2 = (f32[]{:T(128)}, f32[96,384,128,1]{1,2,3,0:T(8,128)}) fusion(f32[96,128]{1,0:T(8,128)S(1)} %broadcast_divide_fusion, bf16[96,5,128,128]{3,2,1,0:T(8,128)(2,1)} %all-gather.7.cloned.1.call-done, bf16[96,5,384,128]{3,2,1,0:T(8,128)(2,1)} %bitcast.89, pred[96,5]{1,0:T(8,128)(4,1)S(1)} %copy.32), kind=kOutput, calls=%fused_computation.37 | convolution fusion | flops 6082265088 | bytes 81838560 | tf_op jit(solution)/shard_map/cisk,isok->cio/dot_general | solution.py:23
  767.7 11.8 multiply_convert_fusion.2
  779.5 5.1 all-to-all-start.1
  784.6 0.0 all-gather.9.cloned.1.call-start
  784.6 220.6 %all-reduce = (f32[]{:T(128)}, f32[]{:T(128)}) all-reduce(f32[]{:T(128)} %get-tuple-element.11, f32[]{:T(128)} %get-tuple-element.9), channel_id=1, replica_groups=mesh['row'=8,'col'=4] {'row','col'}, use_global_device_ids=true, to_apply=%region_3.6 | all-reduce | flops 2 | bytes 16 | tf_op jit(solution)/shard_map/psum | solution.py:50
  1006.5 0.0 all-to-all-done.1
  1006.5 12.4 multiply_bitcast_fusion.1
  1018.9 7.6 copy.52
  1026.5 12.7 fusion.21
  1039.2 0.0 all-gather.9.cloned.1.call-update
  1039.2 227.3 %all-gather.9.cloned.1.call-done = bf16[12288,1536]{0,1:T(8,128)(2,1)} async-done(((bf16[3072,1536]{0,1:T(8,128)(2,1)}), bf16[12288,1536]{0,1:T(8,128)(2,1)}) %all-gather.9.cloned.1.call-update) | async-done | bytes 37748752 | tf_op jit(solution)/shard_map/all_gather | solution.py:44
  1266.6 48.7 %copy.42 = bf16[12288,1536]{1,0:T(8,128)(2,1)} copy(bf16[12288,1536]{0,1:T(8,128)(2,1)} %all-gather.9.cloned.1.call-done) | data formatting | bytes 75497472 | tf_op jit(solution)/shard_map/all_gather | solution.py:44
  1315.2 33.3 %gather_fusion.2 = bf16[120,128,1536]{2,1,0:T(8,128)(2,1)} fusion(bf16[96,128,1536]{2,1,0:T(8,128)(2,1)} %bitcast.86, s32[1024]{0:T(1024)S(1)} %copy-done.5), kind=kCustom, calls=%fused_computation.2.clone | custom fusion | bytes 94372320 | tf_op jit(solution)/shard_map/jit(_take)/gather | solution.py:13
  1348.5 24.3 %fusion.5 = f32[24,1536,128,1]{1,2,3,0:T(8,128)} fusion(bf16[24,5,128,128]{3,2,1,0:T(8,128)(2,1)} %param.12, bf16[24,5,128,1536]{3,2,1,0:T(8,128)(2,1)} %bitcast.92, pred[24,5]{1,0:T(8,128)(4,1)S(1)} %copy-done.15), kind=kOutput, calls=%fused_computation.9 | convolution fusion | flops 6063390720 | bytes 69992568 | tf_op jit(solution)/shard_map/jsoi,jsin->jon/dot_general | solution.py:14
  1372.8 18.7 copy.44
  1391.5 7.6 multiply_convert_fusion.1
  1399.1 212.8 %all_to_all.46 = bf16[8,384,1536]{1,2,0:T(8,128)(2,1)} all-to-all(bf16[8,384,1536]{1,2,0:T(8,128)(2,1)S(1)} %multiply_convert_fusion.1), channel_id=1, replica_groups=mesh['row'=8,'col'=4] {'row'}, dimensions={0} | all-to-all | bytes 18874368 | tf_op jit(solution)/shard_map/all_to_all | solution.py:46
  1611.9 12.6 copy.46
  1624.5 23.7 %gather_fusion.3 = bf16[480,384,128]{2,1,0:T(8,128)(2,1)} fusion(bf16[384,96,128]{2,0,1:T(8,128)(2,1)} %copy.46, s32[1024]{0:T(1024)S(1)} %copy-done.1), kind=kCustom, calls=%fused_computation.3.clone | custom fusion | bytes 94373760 | tf_op jit(solution)/shard_map/jit(_take)/gather | solution.py:22
  1648.2 0.0 copy-done.7
  1648.2 31.3 %convert_reduce_fusion.1 = (f32[]{:T(128)}, f32[96,384,128,1]{1,2,3,0:T(8,128)}) fusion(f32[96,128]{1,0:T(8,128)S(1)} %copy-done.7, bf16[96,5,128,128]{3,2,1,0:T(8,128)(2,1)} %all-gather.7.cloned.1.call-done, bf16[96,5,384,128]{3,2,1,0:T(8,128)(2,1)} %bitcast.88, pred[96,5]{1,0:T(8,128)(4,1)S(1)} %copy-done.12), kind=kOutput, calls=%fused_computation.33 | convolution fusion | flops 6082265088 | bytes 81838560 | tf_op jit(solution)/shard_map/cisk,isok->cio/dot_general | solution.py:23
  1679.5 11.8 multiply_convert_fusion
  1691.3 5.1 all-to-all-start.3
  1696.4 226.1 %psum.23 = f32[]{:T(128)} all-reduce(f32[]{:T(128)} %get-tuple-element.13), channel_id=1, replica_groups=mesh['row'=8,'col'=4] {'row','col'}, use_global_device_ids=true, to_apply=%region_7.10 | all-reduce | flops 1 | bytes 8 | tf_op jit(solution)/shard_map/psum | solution.py:50
  1923.2 0.0 all-to-all-done.3
  1923.2 12.4 multiply_bitcast_fusion
  1935.5 7.6 copy.53
  1943.1 15.5 fusion.23
  (32 shorter events, 0.1 us)
Async XLA Ops:
  6.5 20.8 %copy-start.10 = (s32[24,5]{0,1:T(8,128)S(1)}, s32[24,5]{0,1:T(8,128)}, u32[]{:S(2)}) copy-start(s32[24,5]{0,1:T(8,128)} %param.13) | copy-start | bytes 1444
  6.5 250.1 %all-gather.5.cloned.1.call-start = ((), (), s32[]{:S(2)}) async-start(), calls=%async_computation.4 | async-start | bytes 47185920 | tf_op jit(solution)/shard_map/all_gather | solution.py:44
  26.6 666.9 %all-gather.7.cloned.1.call-start = ((), (), s32[]{:S(2)}) async-start(), calls=%async_computation.5 | async-start | bytes 17694720 | tf_op jit(solution)/shard_map/all_gather | solution.py:35
  27.4 311.4 %copy-start.14 = (pred[24,5]{1,0:T(8,128)(4,1)}, pred[24,5]{1,0:T(8,128)(4,1)S(1)}, u32[]{:S(2)}) copy-start(pred[24,5]{1,0:T(8,128)(4,1)S(1)} %copy.33) | copy-start | bytes 364
  30.4 353.5 %copy-start.8 = (f32[8,384]{1,0:T(8,128)}, f32[8,384]{1,0:T(8,128)S(1)}, u32[]{:S(2)}) copy-start(f32[8,384]{1,0:T(8,128)S(1)} %div.47) | copy-start | bytes 36868
  30.4 275.1 %copy-start.4 = (s32[1024]{0:T(1024)}, s32[1024]{0:T(1024)S(1)}, u32[]{:S(2)}) copy-start(s32[1024]{0:T(1024)S(1)} %pad_clamp_fusion.1) | copy-start | bytes 12292
  383.9 16.9 copy-start.13
  395.4 304.7 %all-to-all-start = ((bf16[8,384,1536]{1,2,0:T(8,128)(2,1)}), bf16[8,384,1536]{1,2,0:T(8,128)(2,1)}, u32[]{:S(2)}, u32[]{:S(2)}) async-start(bf16[8,384,1536]{1,2,0:T(8,128)(2,1)} %multiply_convert_fusion.3), calls=%async_computation | async-start | bytes 18874368 | tf_op jit(solution)/shard_map/all_to_all | solution.py:46
  693.1 43.3 %copy-start.11 = (pred[96,5]{1,0:T(8,128)(4,1)}, pred[96,5]{1,0:T(8,128)(4,1)S(1)}, u32[]{:S(2)}) copy-start(pred[96,5]{1,0:T(8,128)(4,1)S(1)} %copy.32) | copy-start | bytes 1444
  693.4 43.0 %copy-start = (s32[1024]{0:T(1024)}, s32[1024]{0:T(1024)S(1)}, u32[]{:S(2)}) copy-start(s32[1024]{0:T(1024)S(1)} %pad_clamp_fusion) | copy-start | bytes 12292
  700.1 36.3 %copy-start.6 = (f32[96,128]{1,0:T(8,128)}, f32[96,128]{1,0:T(8,128)S(1)}, u32[]{:S(2)}) copy-start(f32[96,128]{1,0:T(8,128)S(1)} %broadcast_divide_fusion) | copy-start | bytes 147460
  700.1 67.6 %copy-start.2 = (f32[8,1536]{1,0:T(8,128)}, f32[8,1536]{1,0:T(8,128)S(1)}, u32[]{:S(2)}) copy-start(f32[8,1536]{1,0:T(8,128)S(1)} %div.50) | copy-start | bytes 147460
  779.5 227.0 %all-to-all-start.1 = ((bf16[384,8,1536]{0,2,1:T(8,128)(2,1)}), bf16[384,8,1536]{0,2,1:T(8,128)(2,1)}, u32[]{:S(2)}, u32[]{:S(2)}) async-start(bf16[384,8,1536]{0,2,1:T(8,128)(2,1)} %multiply_convert_fusion.2), calls=%async_computation.1 | async-start | bytes 18874368 | tf_op jit(solution)/shard_map/all_to_all | solution.py:49
  784.6 482.0 %all-gather.9.cloned.1.call-start = ((), (), s32[]{:S(2)}) async-start(), calls=%async_computation.6 | async-start | bytes 47185920 | tf_op jit(solution)/shard_map/all_gather | solution.py:44
  1039.2 276.0 %copy-start.5 = (s32[1024]{0:T(1024)S(1)}, s32[1024]{0:T(1024)}, u32[]{:S(2)}) copy-start(s32[1024]{0:T(1024)} %copy-done.4) | copy-start | bytes 12292
  1315.2 33.3 %copy-start.15 = (pred[24,5]{1,0:T(8,128)(4,1)S(1)}, pred[24,5]{1,0:T(8,128)(4,1)}, u32[]{:S(2)}) copy-start(pred[24,5]{1,0:T(8,128)(4,1)} %copy-done.14) | copy-start | bytes 364
  1372.8 18.7 copy-start.9
  1399.1 225.5 %copy-start.1 = (s32[1024]{0:T(1024)S(1)}, s32[1024]{0:T(1024)}, u32[]{:S(2)}) copy-start(s32[1024]{0:T(1024)} %copy-done) | copy-start | bytes 12292
  1624.5 23.7 %copy-start.7 = (f32[96,128]{1,0:T(8,128)S(1)}, f32[96,128]{1,0:T(8,128)}, u32[]{:S(2)}) copy-start(f32[96,128]{1,0:T(8,128)} %copy-done.6) | copy-start | bytes 147460
  1624.5 23.7 %copy-start.12 = (pred[96,5]{1,0:T(8,128)(4,1)S(1)}, pred[96,5]{1,0:T(8,128)(4,1)}, u32[]{:S(2)}) copy-start(pred[96,5]{1,0:T(8,128)(4,1)} %copy-done.11) | copy-start | bytes 1444
  1648.2 31.3 %copy-start.3 = (f32[8,1536]{1,0:T(8,128)S(1)}, f32[8,1536]{1,0:T(8,128)}, u32[]{:S(2)}) copy-start(f32[8,1536]{1,0:T(8,128)} %copy-done.2) | copy-start | bytes 147460
  1691.3 231.9 %all-to-all-start.3 = ((bf16[384,8,1536]{0,2,1:T(8,128)(2,1)}), bf16[384,8,1536]{0,2,1:T(8,128)(2,1)}, u32[]{:S(2)}, u32[]{:S(2)}) async-start(bf16[384,8,1536]{0,2,1:T(8,128)(2,1)} %multiply_convert_fusion), calls=%async_computation.3 | async-start | bytes 18874368 | tf_op jit(solution)/shard_map/all_to_all | solution.py:49
Sparse Core Ops, SparseCore 0:
  26.7 229.8 all-gather.4
  258.8 288.7 all-gather.6
  1039.4 227.1 all-gather.8
where the time goes:
time: 1970 us
  blocking collectives  952 us (48%)
  waiting for transfers between devices  454 us (23%)
  local copies, waits for them, and re-layouts  290 us (15%)
  other arithmetic  125 us (6%)
  matrix products  113 us (6%)
    all_gather x2, waiting for transfers between devices, local(): gathered = lax.all_gather(current, 'col', axis=0, tiled=True)  454 us
    psum x2, blocking collectives, local(): slab_sum = lax.psum(partial_value, ('row', 'col'))  447 us
    all_gather x1, blocking collectives, local(): lax.all_gather(columns_first, 'row', axis=0, tiled=True)  292 us
    all_to_all x1, blocking collectives, local(): lax.all_to_all(mixed_cols, 'row', split_axis=0, concat_axis=1, tiled=True)  213 us
    all_gather x2, local copies, waits for them, and re-layouts, local(): gathered = lax.all_gather(current, 'col', axis=0, tiled=True)  97.6 us
    gather x2, local copies, waits for them, and re-layouts, second_product(): picked = jnp.take(blocks, columns, axis=0)  66.5 us
    dot_general x2, matrix products, first_product(): jnp.einsum('cisk,isok->cio', picked, tile_set, preferred_element_type=jnp...  62.6 us
    dot_general x2, matrix products, second_product(): jnp.einsum('jsoi,jsin->jon', tile_set, picked, preferred_element_type=jnp...  50.7 us
  transfers between devices with their start and end apart: 6, of which 2 were waited for; matrix products, arithmetic and copies ran while one was open for 8% of the time, Pallas kernels for 0%

commit v1 on v0

--- a/solution.py
+++ b/solution.py
@@ -43,7 +43,12 @@
         current = current_state.astype(jnp.bfloat16)
         gathered = lax.all_gather(current, "col", axis=0, tiled=True)
         mixed_cols = second_product(gathered, tiles_second, columns_second, inverse_second)
-        slab_data = lax.all_to_all(mixed_cols, "row", split_axis=0, concat_axis=1, tiled=True)
+        slab_data = jnp.concatenate(
+            lax.all_to_all(
+                jnp.stack(jnp.split(mixed_cols, lax.axis_size("row"), axis=0)), "row", 0, 0
+            ),
+            axis=1,
+        )
         propagated = first_product(slab_data, all_first, all_columns, inverse_first)
         partial_value = jnp.sum(propagated.astype(jnp.float32))
         returned = lax.all_to_all(propagated, "row", split_axis=1, concat_axis=0, tiled=True)

time: 1970 us -> 1970 us (level)
    another operation x0 -> x4, local copies, waits for them, and re-layouts: none -> 26.7 us  [the longest x2 25.2 us: first_product(): blocks = slab_data.reshape(slab_data.shape[0], -1, tile_size)]
    reshape x2 -> x0, local copies, waits for them, and re-layouts: 25.2 us -> none  [first_product(): blocks = slab_data.reshape(slab_data.shape[0], -1, tile_size)]
where the time goes in v1:
time: 1970 us
  blocking collectives  946 us (48%)
  waiting for transfers between devices  454 us (23%)
  local copies, waits for them, and re-layouts  302 us (15%)
  other arithmetic  121 us (6%)
  matrix products  113 us (6%)
    all_gather x2, waiting for transfers between devices, local(): gathered = lax.all_gather(current, 'col', axis=0, tiled=True)  454 us
    psum x2, blocking collectives, local(): slab_sum = lax.psum(partial_value, ('row', 'col'))  447 us
    all_gather x1, blocking collectives, local(): lax.all_gather(columns_first, 'row', axis=0, tiled=True)  286 us
    all_to_all x1, blocking collectives, local(): lax.all_to_all(jnp.stack(jnp.split(mixed_cols, lax.axis_size('row'), axis...  213 us
    all_gather x2, local copies, waits for them, and re-layouts, local(): gathered = lax.all_gather(current, 'col', axis=0, tiled=True)  97.6 us
    gather x2, local copies, waits for them, and re-layouts, second_product(): picked = jnp.take(blocks, columns, axis=0)  66.5 us
    dot_general x2, matrix products, first_product(): jnp.einsum('cisk,isok->cio', picked, tile_set, preferred_element_type=jnp...  62.6 us
    dot_general x2, matrix products, second_product(): jnp.einsum('jsoi,jsin->jon', tile_set, picked, preferred_element_type=jnp...  50.7 us
  transfers between devices with their start and end apart: 6, of which 2 were waited for; matrix products, arithmetic and copies ran while one was open for 8% of the time, Pallas kernels for 0%

profile of v1, /device:TPU:0, one launch (start us, length us, event | category | flops | bytes accessed | tf_op | source)
XLA Modules:
  0.0 1967.5 jit_solution(2612123066868449828)
XLA Ops:
  6.5 20.0 %fusion.44 = (f32[]{:T(128)}, bf16[3072,1536]{0,1:T(8,128)(2,1)}) fusion(f32[1536,3072]{1,0:T(8,128)} %param.9), kind=kLoop, calls=%fused_computation.87 | loop fusion | flops 9437183 | bytes 28311556 | tf_op jit(solution)/shard_map/reduce_sum | solution.py:40
  26.5 0.0 all-gather.5.cloned.1.call-update
  26.6 0.0 all-gather.7.cloned.1.call-start
  26.6 0.7 all-gather.7.cloned.1.call-update
  27.3 0.1 copy.33
  27.5 0.1 copy.37
  27.5 0.1 reshape.134
  27.7 2.7 convert_reduce_fusion.3
  30.4 226.2 %all-gather.5.cloned.1.call-done = bf16[12288,1536]{0,1:T(8,128)(2,1)} async-done(((bf16[3072,1536]{0,1:T(8,128)(2,1)}), bf16[12288,1536]{0,1:T(8,128)(2,1)}) %all-gather.5.cloned.1.call-update) | async-done | bytes 37748752 | tf_op jit(solution)/shard_map/all_gather | solution.py:44
  256.6 48.9 %copy.36 = bf16[12288,1536]{1,0:T(8,128)(2,1)} copy(bf16[12288,1536]{0,1:T(8,128)(2,1)} %all-gather.5.cloned.1.call-done) | data formatting | bytes 75497472 | tf_op jit(solution)/shard_map/all_gather | solution.py:44
  305.5 33.3 %gather_fusion = bf16[120,128,1536]{2,1,0:T(8,128)(2,1)} fusion(bf16[96,128,1536]{2,1,0:T(8,128)(2,1)} %bitcast.153, s32[1024]{0:T(1024)S(1)} %pad_clamp_fusion.1), kind=kCustom, calls=%fused_computation.clone | custom fusion | bytes 94372320 | tf_op jit(solution)/shard_map/jit(_take)/gather | solution.py:13
  338.8 26.4 %fusion.8 = f32[24,1536,128,1]{1,2,3,0:T(8,128)} fusion(bf16[24,5,128,128]{3,2,1,0:T(8,128)(2,1)} %param.12, bf16[24,5,128,1536]{3,2,1,0:T(8,128)(2,1)} %bitcast.159, pred[24,5]{1,0:T(8,128)(4,1)S(1)} %copy.33), kind=kOutput, calls=%fused_computation.12 | convolution fusion | flops 6063390720 | bytes 69992568 | tf_op jit(solution)/shard_map/jsoi,jsin->jon/dot_general | solution.py:14
  365.2 18.7 copy.38
  383.9 7.7 multiply_convert_fusion.3
  391.7 1.2 fusion.39
  392.8 1.2 fusion.38
  394.0 1.2 fusion.37
  395.2 1.2 fusion.36
  396.4 1.2 fusion.35
  397.6 1.2 fusion.34
  398.8 1.2 fusion.33
  399.9 1.2 fusion.32
  401.1 5.5 all-to-all-start
  406.6 286.3 %all-gather = s32[8,12,5]{1,2,0:T(8,128)S(1)} all-gather(s32[1,12,5]{1,2,0:T(8,128)S(1)} %bitcast.165), channel_id=1, replica_groups=mesh['row'=8,'col'=4] {'row'}, dimensions={0}, use_global_device_ids=true | all-gather | bytes 2160 | tf_op jit(solution)/shard_map/all_gather | solution.py:36
  692.9 0.1 reshape.133
  693.0 0.1 copy.32
  693.1 0.1 copy.39
  693.3 0.2 reshape.138
  693.4 0.0 all-gather.7.cloned.1.call-done
  693.5 6.6 convert_reduce_fusion
  700.2 12.6 copy.40
  712.8 23.6 %gather_fusion.1 = bf16[480,384,128]{2,1,0:T(8,128)(2,1)} fusion(bf16[384,96,128]{2,0,1:T(8,128)(2,1)} %copy.40, s32[1024]{0:T(1024)S(1)} %pad_clamp_fusion), kind=kCustom, calls=%fused_computation.1.clone | custom fusion | bytes 94373760 | tf_op jit(solution)/shard_map/jit(_take)/gather | solution.py:22
  736.4 31.3 %convert_reduce_fusion.2 = (f32[]{:T(128)}, f32[96,384,128,1]{1,2,3,0:T(8,128)}) fusion(f32[96,128]{1,0:T(8,128)S(1)} %broadcast_divide_fusion, bf16[96,5,128,128]{3,2,1,0:T(8,128)(2,1)} %all-gather.7.cloned.1.call-done, bf16[96,5,384,128]{3,2,1,0:T(8,128)(2,1)} %bitcast.155, pred[96,5]{1,0:T(8,128)(4,1)S(1)} %copy.32), kind=kOutput, calls=%fused_computation.37 | convolution fusion | flops 6082265088 | bytes 81838560 | tf_op jit(solution)/shard_map/cisk,isok->cio/dot_general | solution.py:23
  767.7 11.8 multiply_convert_fusion.2
  779.5 5.1 all-to-all-start.1
  784.6 0.0 all-gather.9.cloned.1.call-start
  784.6 220.6 %all-reduce = (f32[]{:T(128)}, f32[]{:T(128)}) all-reduce(f32[]{:T(128)} %get-tuple-element.11, f32[]{:T(128)} %get-tuple-element.9), channel_id=1, replica_groups=mesh['row'=8,'col'=4] {'row','col'}, use_global_device_ids=true, to_apply=%region_3.6 | all-reduce | flops 2 | bytes 16 | tf_op jit(solution)/shard_map/psum | solution.py:55
  1006.5 12.4 multiply_bitcast_fusion.1
  1018.9 7.6 copy.52
  1026.5 12.7 fusion.21
  1039.2 227.3 %all-gather.9.cloned.1.call-done = bf16[12288,1536]{0,1:T(8,128)(2,1)} async-done(((bf16[3072,1536]{0,1:T(8,128)(2,1)}), bf16[12288,1536]{0,1:T(8,128)(2,1)}) %all-gather.9.cloned.1.call-update) | async-done | bytes 37748752 | tf_op jit(solution)/shard_map/all_gather | solution.py:44
  1266.6 48.7 %copy.42 = bf16[12288,1536]{1,0:T(8,128)(2,1)} copy(bf16[12288,1536]{0,1:T(8,128)(2,1)} %all-gather.9.cloned.1.call-done) | data formatting | bytes 75497472 | tf_op jit(solution)/shard_map/all_gather | solution.py:44
  1315.2 33.3 %gather_fusion.2 = bf16[120,128,1536]{2,1,0:T(8,128)(2,1)} fusion(bf16[96,128,1536]{2,1,0:T(8,128)(2,1)} %bitcast.152, s32[1024]{0:T(1024)S(1)} %copy-done.5), kind=kCustom, calls=%fused_computation.2.clone | custom fusion | bytes 94372320 | tf_op jit(solution)/shard_map/jit(_take)/gather | solution.py:13
  1348.5 24.3 %fusion.5 = f32[24,1536,128,1]{1,2,3,0:T(8,128)} fusion(bf16[24,5,128,128]{3,2,1,0:T(8,128)(2,1)} %param.12, bf16[24,5,128,1536]{3,2,1,0:T(8,128)(2,1)} %bitcast.158, pred[24,5]{1,0:T(8,128)(4,1)S(1)} %copy-done.15), kind=kOutput, calls=%fused_computation.9 | convolution fusion | flops 6063390720 | bytes 69992568 | tf_op jit(solution)/shard_map/jsoi,jsin->jon/dot_general | solution.py:14
  1372.8 18.7 copy.44
  1391.5 7.7 multiply_convert_fusion.1
  1399.2 0.2 fusion.31
  1399.3 0.3 fusion.30
  1399.6 0.3 fusion.29
  1399.9 0.3 fusion.28
  1400.2 0.3 fusion.27
  1400.5 0.3 fusion.26
  1400.8 0.3 fusion.25
  1401.1 0.3 fusion.24
  1401.3 212.8 %all_to_all.30 = bf16[8,384,1536]{1,2,0:T(8,128)(2,1)} all-to-all(bf16[8,384,1536]{1,2,0:T(8,128)(2,1)S(1)} %fusion.24), channel_id=1, replica_groups=mesh['row'=8,'col'=4] {'row'}, dimensions={0} | all-to-all | bytes 18874368 | tf_op jit(solution)/shard_map/all_to_all | solution.py:47
  1614.2 12.6 copy.46
  1626.8 23.7 %gather_fusion.3 = bf16[480,384,128]{2,1,0:T(8,128)(2,1)} fusion(bf16[384,96,128]{2,0,1:T(8,128)(2,1)} %copy.46, s32[1024]{0:T(1024)S(1)} %copy-done.1), kind=kCustom, calls=%fused_computation.3.clone | custom fusion | bytes 94373760 | tf_op jit(solution)/shard_map/jit(_take)/gather | solution.py:22
  1650.5 31.3 %convert_reduce_fusion.1 = (f32[]{:T(128)}, f32[96,384,128,1]{1,2,3,0:T(8,128)}) fusion(f32[96,128]{1,0:T(8,128)S(1)} %copy-done.7, bf16[96,5,128,128]{3,2,1,0:T(8,128)(2,1)} %all-gather.7.cloned.1.call-done, bf16[96,5,384,128]{3,2,1,0:T(8,128)(2,1)} %bitcast.154, pred[96,5]{1,0:T(8,128)(4,1)S(1)} %copy-done.12), kind=kOutput, calls=%fused_computation.33 | convolution fusion | flops 6082265088 | bytes 81838560 | tf_op jit(solution)/shard_map/cisk,isok->cio/dot_general | solution.py:23
  1681.8 11.8 multiply_convert_fusion
  1693.6 5.1 all-to-all-start.3
  1698.7 226.1 %psum.23 = f32[]{:T(128)} all-reduce(f32[]{:T(128)} %get-tuple-element.13), channel_id=1, replica_groups=mesh['row'=8,'col'=4] {'row','col'}, use_global_device_ids=true, to_apply=%region_7.10 | all-reduce | flops 1 | bytes 8 | tf_op jit(solution)/shard_map/psum | solution.py:55
  1925.5 12.4 multiply_bitcast_fusion
  1937.8 7.6 copy.53
  1945.4 15.5 fusion.23
  (47 shorter events, 0.2 us)
Async XLA Ops:
  6.5 250.1 %all-gather.5.cloned.1.call-start = ((), (), s32[]{:S(2)}) async-start(), calls=%async_computation.4 | async-start | bytes 47185920 | tf_op jit(solution)/shard_map/all_gather | solution.py:44
  26.5 0.8 copy-start.10
  26.6 666.9 %all-gather.7.cloned.1.call-start = ((), (), s32[]{:S(2)}) async-start(), calls=%async_computation.5 | async-start | bytes 17694720 | tf_op jit(solution)/shard_map/all_gather | solution.py:35
  27.4 311.4 %copy-start.14 = (pred[24,5]{1,0:T(8,128)(4,1)}, pred[24,5]{1,0:T(8,128)(4,1)S(1)}, u32[]{:S(2)}) copy-start(pred[24,5]{1,0:T(8,128)(4,1)S(1)} %copy.33) | copy-start | bytes 364
  27.7 277.9 %copy-start.4 = (s32[1024]{0:T(1024)}, s32[1024]{0:T(1024)S(1)}, u32[]{:S(2)}) copy-start(s32[1024]{0:T(1024)S(1)} %pad_clamp_fusion.1) | copy-start | bytes 12292
  30.4 353.5 %copy-start.8 = (f32[3072]{0:T(1024)}, f32[3072]{0:T(1024)S(1)}, u32[]{:S(2)}) copy-start(f32[3072]{0:T(1024)S(1)} %divide_bitcast_fusion) | copy-start | bytes 36868
  401.1 5.5 copy-start.13
  401.1 299.0 %all-to-all-start = ((bf16[8,384,1536]{1,2,0:T(8,128)(2,1)}), bf16[8,384,1536]{1,2,0:T(8,128)(2,1)}, u32[]{:S(2)}, u32[]{:S(2)}) async-start(bf16[8,384,1536]{1,2,0:T(8,128)(2,1)} %fusion.32), calls=%async_computation | async-start | bytes 18874368 | tf_op jit(solution)/shard_map/all_to_all | solution.py:47
  693.1 43.3 %copy-start.11 = (pred[96,5]{1,0:T(8,128)(4,1)}, pred[96,5]{1,0:T(8,128)(4,1)S(1)}, u32[]{:S(2)}) copy-start(pred[96,5]{1,0:T(8,128)(4,1)S(1)} %copy.32) | copy-start | bytes 1444
  693.4 19.3 copy-start
  700.1 36.3 %copy-start.6 = (f32[96,128]{1,0:T(8,128)}, f32[96,128]{1,0:T(8,128)S(1)}, u32[]{:S(2)}) copy-start(f32[96,128]{1,0:T(8,128)S(1)} %broadcast_divide_fusion) | copy-start | bytes 147460
  700.1 67.5 %copy-start.2 = (f32[8,1536]{1,0:T(8,128)}, f32[8,1536]{1,0:T(8,128)S(1)}, u32[]{:S(2)}) copy-start(f32[8,1536]{1,0:T(8,128)S(1)} %div.50) | copy-start | bytes 147460
  779.5 227.0 %all-to-all-start.1 = ((bf16[384,8,1536]{0,2,1:T(8,128)(2,1)}), bf16[384,8,1536]{0,2,1:T(8,128)(2,1)}, u32[]{:S(2)}, u32[]{:S(2)}) async-start(bf16[384,8,1536]{0,2,1:T(8,128)(2,1)} %multiply_convert_fusion.2), calls=%async_computation.1 | async-start | bytes 18874368 | tf_op jit(solution)/shard_map/all_to_all | solution.py:54
  784.6 482.0 %all-gather.9.cloned.1.call-start = ((), (), s32[]{:S(2)}) async-start(), calls=%async_computation.6 | async-start | bytes 47185920 | tf_op jit(solution)/shard_map/all_gather | solution.py:44
  1039.2 276.0 %copy-start.5 = (s32[1024]{0:T(1024)S(1)}, s32[1024]{0:T(1024)}, u32[]{:S(2)}) copy-start(s32[1024]{0:T(1024)} %copy-done.4) | copy-start | bytes 12292
  1315.2 33.3 %copy-start.15 = (pred[24,5]{1,0:T(8,128)(4,1)S(1)}, pred[24,5]{1,0:T(8,128)(4,1)}, u32[]{:S(2)}) copy-start(pred[24,5]{1,0:T(8,128)(4,1)} %copy-done.14) | copy-start | bytes 364
  1372.8 18.7 copy-start.9
  1614.2 12.6 copy-start.1
  1626.8 23.7 %copy-start.7 = (f32[96,128]{1,0:T(8,128)S(1)}, f32[96,128]{1,0:T(8,128)}, u32[]{:S(2)}) copy-start(f32[96,128]{1,0:T(8,128)} %copy-done.6) | copy-start | bytes 147460
  1626.8 23.7 %copy-start.12 = (pred[96,5]{1,0:T(8,128)(4,1)S(1)}, pred[96,5]{1,0:T(8,128)(4,1)}, u32[]{:S(2)}) copy-start(pred[96,5]{1,0:T(8,128)(4,1)} %copy-done.11) | copy-start | bytes 1444
  1650.5 31.3 %copy-start.3 = (f32[8,1536]{1,0:T(8,128)S(1)}, f32[8,1536]{1,0:T(8,128)}, u32[]{:S(2)}) copy-start(f32[8,1536]{1,0:T(8,128)} %copy-done.2) | copy-start | bytes 147460
  1693.6 231.9 %all-to-all-start.3 = ((bf16[384,8,1536]{0,2,1:T(8,128)(2,1)}), bf16[384,8,1536]{0,2,1:T(8,128)(2,1)}, u32[]{:S(2)}, u32[]{:S(2)}) async-start(bf16[384,8,1536]{0,2,1:T(8,128)(2,1)} %multiply_convert_fusion), calls=%async_computation.3 | async-start | bytes 18874368 | tf_op jit(solution)/shard_map/all_to_all | solution.py:54
Sparse Core Ops, SparseCore 0:
  26.7 229.8 all-gather.4
  258.8 365.1 all-gather.6
  1039.3 227.1 all-gather.8
